TPU v7x, 32 devices: a whole 2x2x4 slice. The times are simulated.
32 devices in a mesh: groups: 2 (over y), fsdp: 4 (over z), mp: 2 (over x), sub: 2 (over core).
Axes of the slice: x: 2, y: 2, z: 4, core: 2. Of those that a mesh axis runs over, the one named last changes fastest.
Arguments:
- hidden: bfloat16 [128, 36864], P(('groups', 'fsdp', 'sub'), 'mp'), parts along dimension 0, may hold values from -6 to 6
- residual: bfloat16 [128, 4608], P(('groups', 'fsdp', 'sub')), parts along dimension 0, may hold values from -6 to 6
- down_packed: int32 [4608, 4608], P('mp', 'fsdp'), may hold values from -2147483648 to 2147483646
- down_scale: bfloat16 [288, 4608], P('mp', 'fsdp'), may hold values from 0.00049972534 to 0.0019989014
- post_gain: float32 [4608], replicated, may hold values from 0.1 to 1.9
- final_gain: float32 [4608], replicated, may hold values from 0.1 to 1.9
- embed_packed: int32 [8192, 576], P(('fsdp', 'mp', 'sub')), may hold values from -2147483648 to 2147483646
- embed_scale: bfloat16 [8192, 36], P(('fsdp', 'mp', 'sub')), may hold values from 0.0059814453 to 0.029907227
- targets: int32 [128], P(('groups', 'fsdp', 'sub')), parts along dimension 0, may hold values from 0 to 8191
- loss_mask: int32 [128], P(('groups', 'fsdp', 'sub')), parts along dimension 0, may hold values 0 or 1
Outputs:
- token_loss: float32 [128], P(('groups', 'fsdp', 'sub')), parts along dimension 0
- mean_loss: float32 [2], P('groups'), parts along dimension 0
There are 2 independent parts, one for each index of `groups`. A program takes and returns all parts, laid end to end along the dimension named above; an argument that names none is the same for every part. Nothing has to cross between parts.
Inputs may be any that keep to these rules, and one draw needn't show every extreme that they name: `down_packed`: bits 4 k to 4 k + 3 of the word in row r hold the signed code of row 8 r + k of the down projection, k = 0..7. `embed_packed`: bits 4 k to 4 k + 3 of the word in column j hold the signed code of column k * 576 + j of the embedding, k = 0..7.
All inputs are finite; a program needn't handle non-finite values. No bound on the sum of `loss_mask` on one device may be relied on, other than what follows from the above.
Results may differ from a plain program's by a relative error of at most 0.00097.
Values may be sent and summed in bfloat16 or wider, within the bound.
A program may use at most 128 MiB of HBM per device.

v0:
```python
import jax
import jax.numpy as jnp
from jax import lax
from jax.sharding import PartitionSpec as P

EPS = 1e-06
CAP = 30.0


def signed_planes(words):
    shifts = (28 - 4 * jnp.arange(8, dtype=jnp.int32))[None, :, None]
    lifted = jnp.left_shift(words[:, None, :], shifts)
    return jnp.right_shift(lifted, 28)


def dequant_down(words, scales):
    cols = words.shape[1]
    codes = signed_planes(words).astype(jnp.bfloat16)
    grouped = codes.reshape(scales.shape[0], -1, cols) * scales[:, None, :]
    return grouped.reshape(-1, cols)


def dequant_embed(words, scales):
    rows = words.shape[0]
    codes = signed_planes(words).astype(jnp.bfloat16)
    grouped = codes.reshape(rows, scales.shape[1], -1) * scales[:, :, None]
    return grouped.reshape(rows, -1)


def normalize_rows(ffn, residual, post_gain, final_gain):
    ffn = lax.psum(ffn, "mp")
    normed = ffn * lax.rsqrt(jnp.mean(ffn * ffn, axis=-1, keepdims=True) + EPS) * post_gain
    stream = residual.astype(jnp.float32) + normed
    return (
        stream * lax.rsqrt(jnp.mean(stream * stream, axis=-1, keepdims=True) + EPS) * final_gain
    ).astype(jnp.bfloat16)


def on_device(
    hidden,
    residual,
    down_packed,
    down_scale,
    post_gain,
    final_gain,
    embed_packed,
    embed_scale,
    targets,
    loss_mask,
):
    tok_rows = hidden.shape[0]
    local_weight = dequant_down(down_packed, down_scale)
    partial_cols = jnp.dot(
        lax.all_gather(hidden, "fsdp", axis=0, tiled=True),
        local_weight,
        preferred_element_type=jnp.float32,
    )
    ffn = lax.all_to_all(partial_cols, "fsdp", split_axis=0, concat_axis=1, tiled=True)
    states = normalize_rows(ffn, residual, post_gain, final_gain)
    all_states, all_targets = (
        lax.all_gather(states, ("fsdp", "sub"), axis=0, tiled=True),
        lax.all_gather(targets, ("fsdp", "sub"), axis=0, tiled=True),
    )
    embed = dequant_embed(embed_packed, embed_scale)
    logits = lax.dot_general(
        all_states, embed, (((1,), (1,)), ((), ())), preferred_element_type=jnp.float32
    )
    capped = CAP * jnp.tanh(logits / CAP)
    vocab_rows = embed.shape[0]
    first_id = lax.axis_index(("fsdp", "mp", "sub")) * vocab_rows
    ids = first_id + jnp.arange(vocab_rows, dtype=jnp.int32)
    hits = all_targets[:, None] == ids[None, :]
    exp_sums, target_logits = lax.psum(
        (jnp.sum(jnp.exp(capped), axis=1), jnp.sum(jnp.where(hits, capped, 0.0), axis=1)),
        ("fsdp", "mp", "sub"),
    )
    own_start = lax.axis_index(("fsdp", "sub")) * tok_rows
    own_sums = lax.dynamic_slice_in_dim(exp_sums, own_start, tok_rows, 0)
    own_targets = lax.dynamic_slice_in_dim(target_logits, own_start, tok_rows, 0)
    weights = loss_mask.astype(jnp.float32)
    token_loss = weights * (jnp.log(own_sums) - own_targets)
    loss_sum, count = lax.psum((jnp.sum(token_loss), jnp.sum(weights)), ("fsdp", "sub"))
    mean_loss = (loss_sum / jnp.maximum(count, 1.0)).reshape(1)
    return (token_loss, mean_loss)


def solution(mesh):
    return jax.shard_map(
        on_device,
        mesh=mesh,
        in_specs=(
            P(("groups", "fsdp", "sub"), "mp"),
            P(("groups", "fsdp", "sub"), None),
            P("mp", "fsdp"),
            P("mp", "fsdp"),
            P(),
            P(),
            P(("fsdp", "mp", "sub"), None),
            P(("fsdp", "mp", "sub"), None),
            P(("groups", "fsdp", "sub")),
            P(("groups", "fsdp", "sub")),
        ),
        out_specs=(P(("groups", "fsdp", "sub")), P("groups")),
        check_vma=False,
    )
```

profile of v0, /device:TPU:0, one launch (start us, length us, event | category | flops | bytes accessed | tf_op | source)
XLA Modules:
  0.0 167.8 jit_solution(12297695420085963303)
XLA Ops:
  7.2 0.0 all-gather.2.cloned.1.call-start
  7.2 0.7 all-gather.2.cloned.1.call-update
  7.9 0.0 all-reduce.5.cloned.1.call-start
  8.0 0.1 shift_left.49
  8.1 17.8 %fusion.2 = bf16[18432,1152]{1,0:T(8,128)(2,1)} fusion(s32[18432]{0:T(1024)S(1)} %broadcast_bitcast_fusion, s32[2304,1152]{1,0:T(8,128)} %param.12, bf16[144,1152]{1,0:T(8,128)(2,1)} %param.13), kind=kLoop, calls=%fused_computation.3 | loop fusion | flops 148635648 | bytes 53489664 | tf_op jit(solution)/shard_map/mul | solution.py:19
  25.9 0.0 copy-start.7
  25.9 0.0 copy-start.6
  25.9 0.0 copy-start
  25.9 0.0 copy-start.3
  26.0 0.0 copy-start.1
  26.0 0.0 copy-start.2
  26.0 0.0 copy-start.4
  26.0 16.6 %all-gather.2.cloned.1.call-done = bf16[32,18432]{1,0:T(8,128)(2,1)} async-done(((bf16[8,18432]{1,0:T(8,128)(2,1)}), bf16[32,18432]{1,0:T(8,128)(2,1)}) %all-gather.2.cloned.1.call-update) | async-done | bytes 1179664 | tf_op jit(solution)/shard_map/all_gather | solution.py:54
  42.6 15.8 %convolution_bitcast_fusion = f32[4,8,1152]{2,1,0:T(8,128)S(1)} fusion(bf16[32,18432]{1,0:T(8,128)(2,1)} %all-gather.2.cloned.1.call-done, bf16[18432,1152]{1,0:T(8,128)(2,1)} %fusion.2), kind=kOutput, calls=%fused_computation.8 | convolution fusion | flops 1358954496 | bytes 43794432 | tf_op jit(solution)/shard_map/dot_general | solution.py:53
  58.4 0.0 copy-start.5
  58.4 9.7 %all_to_all.19 = f32[4,8,1152]{2,1,0:T(8,128)} all-to-all(f32[4,8,1152]{2,1,0:T(8,128)S(1)} %convolution_bitcast_fusion), channel_id=1, replica_groups=mesh['groups'=2,'fsdp'=4,'mp'=2,'sub'=2] {'fsdp'}, dimensions={0} | all-to-all | bytes 294912 | tf_op jit(solution)/shard_map/all_to_all | solution.py:58
  68.1 0.0 all-reduce.5.cloned.1.call-update
  68.1 0.1 shift_left.56
  68.2 0.1 shift_left.57
  68.3 0.0 copy-done.7
  68.3 0.6 dynamic-slice
  69.5 0.0 copy-done.6
  69.5 0.2 dynamic-update-slice
  69.8 0.0 copy-done
  69.8 0.0 copy-done.3
  69.8 3.6 %fusion.5 = bf16[512,4608]{0,1:T(8,128)(2,1)} fusion(s32[4608]{0:T(1024)S(1)} %shift_left.57, s32[512,576]{0,1:T(8,128)S(1)} %copy-done, bf16[512,36]{0,1:T(8,128)(2,1)S(1)} %copy-done.3), kind=kLoop, calls=%fused_computation.7 | loop fusion | flops 16515072 | bytes 5953536 | tf_op jit(solution)/shard_map/mul | solution.py:26
  73.4 6.5 %all-reduce = s32[64]{0:T(128)S(1)} all-reduce(s32[64]{0:T(128)S(1)} %dynamic-update-slice), channel_id=1, replica_groups=mesh['groups'=2,'fsdp'=4,'mp'=2,'sub'=2] {'fsdp','sub'}, use_global_device_ids=true, to_apply=%add | all-reduce | flops 64 | bytes 512
  79.8 8.8 %all-reduce.5.cloned.1.call-done = f32[8,4608]{1,0:T(8,128)} async-done(((f32[8,4608]{1,0:T(8,128)}), f32[8,4608]{1,0:T(8,128)}) %all-reduce.5.cloned.1.call-update) | async-done | bytes 147472 | tf_op jit(solution)/shard_map/psum | solution.py:31
  88.7 1.1 multiply_reduce_fusion.1
  89.7 0.0 copy-done.1
  89.8 0.0 copy-done.2
  89.8 1.1 multiply_reduce_fusion
  90.9 0.0 copy-done.4
  90.9 1.0 multiply_convert_fusion
  91.9 15.1 %all_gather.10 = bf16[64,4608]{1,0:T(8,128)(2,1)S(1)} all-gather(bf16[8,4608]{1,0:T(8,128)(2,1)S(1)} %multiply_convert_fusion), channel_id=1, replica_groups=mesh['groups'=2,'fsdp'=4,'mp'=2,'sub'=2] {'fsdp','sub'}, dimensions={0}, use_global_device_ids=true | all-gather | bytes 663552 | tf_op jit(solution)/shard_map/all_gather | solution.py:61
  107.0 3.4 %exponential_reduce_fusion = (f32[64]{0:T(128)S(1)}, f32[64]{0:T(128)S(1)}) fusion(s32[512]{0:T(512)S(1)} %iota_add_fusion, s32[64]{0:T(128)S(1)} %all-reduce, bf16[64,4608]{1,0:T(8,128)(2,1)S(1)} %all_gather.10, bf16[512,4608]{0,1:T(8,128)(2,1)} %fusion.5), kind=kOutput, calls=%fused_computation.17 | convolution fusion | flops 302186368 | bytes 5311232 | tf_op jit(solution)/shard_map/dot_general | solution.py:65
  110.4 32.7 %all-reduce.1 = (f32[64]{0:T(128)S(1)}, f32[64]{0:T(128)S(1)}) all-reduce(f32[64]{0:T(128)S(1)} %get-tuple-element.3, f32[64]{0:T(128)S(1)} %get-tuple-element.2), channel_id=1, replica_groups=mesh['groups'=2,'fsdp'=4,'mp'=2,'sub'=2] {'fsdp','mp','sub'}, use_global_device_ids=true, to_apply=%region_6.7 | all-reduce | flops 128 | bytes 1024 | tf_op jit(solution)/shard_map/psum | solution.py:73
  143.1 0.0 copy-done.5
  143.1 1.3 fusion.8
  144.4 14.2 %all-reduce.2 = (f32[]{:T(128)}, f32[]{:T(128)}) all-reduce(f32[]{:T(128)} %get-tuple-element.8, f32[]{:T(128)} %get-tuple-element.10), channel_id=1, replica_groups=mesh['groups'=2,'fsdp'=4,'mp'=2,'sub'=2] {'fsdp','sub'}, use_global_device_ids=true, to_apply=%region_8.9 | all-reduce | flops 2 | bytes 16 | tf_op jit(solution)/shard_map/psum | solution.py:82
  (7 shorter events, 0.0 us)
Async XLA Ops:
  7.2 35.4 %all-gather.2.cloned.1.call-start = ((), (), s32[]{:S(2)}) async-start(), calls=%async_computation.1 | async-start | bytes 1474560 | tf_op jit(solution)/shard_map/all_gather | solution.py:54
  7.9 80.8 %all-reduce.5.cloned.1.call-start = ((), (), s32[]{:S(2)}) async-start(), calls=%async_computation.2 | async-start | bytes 294912 | tf_op jit(solution)/shard_map/psum | solution.py:31
  25.9 42.4 %copy-start.7 = (u32[32]{0:T(128)S(1)}, u32[32]{0:T(128)}, u32[]{:S(2)}) copy-start(u32[32]{0:T(128)} %constant.48) | copy-start | bytes 388
  25.9 43.6 %copy-start.6 = (s32[8]{0:T(128)S(1)}, s32[8]{0:T(128)}, u32[]{:S(2)}) copy-start(s32[8]{0:T(128)} %param.18) | copy-start | bytes 100
  25.9 43.9 %copy-start = (s32[512,576]{0,1:T(8,128)S(1)}, s32[512,576]{0,1:T(8,128)}, u32[]{:S(2)}) copy-start(s32[512,576]{0,1:T(8,128)} %param.16) | copy-start | bytes 3538948
  25.9 43.8 %copy-start.3 = (bf16[512,36]{0,1:T(8,128)(2,1)S(1)}, bf16[512,36]{0,1:T(8,128)(2,1)}, u32[]{:S(2)}) copy-start(bf16[512,36]{0,1:T(8,128)(2,1)} %param.17) | copy-start | bytes 110596
  26.0 63.8 %copy-start.1 = (bf16[8,4608]{1,0:T(8,128)(2,1)S(1)}, bf16[8,4608]{1,0:T(8,128)(2,1)}, u32[]{:S(2)}) copy-start(bf16[8,4608]{1,0:T(8,128)(2,1)} %param.11) | copy-start | bytes 221188
  26.0 63.8 %copy-start.2 = (f32[4608]{0:T(1024)S(1)}, f32[4608]{0:T(1024)}, u32[]{:S(2)}) copy-start(f32[4608]{0:T(1024)} %param.14) | copy-start | bytes 55300
  26.0 64.9 %copy-start.4 = (f32[4608]{0:T(1024)S(1)}, f32[4608]{0:T(1024)}, u32[]{:S(2)}) copy-start(f32[4608]{0:T(1024)} %param.15) | copy-start | bytes 55300
  58.4 84.8 %copy-start.5 = (s32[8]{0:T(128)S(1)}, s32[8]{0:T(128)}, u32[]{:S(2)}) copy-start(s32[8]{0:T(128)} %param.19) | copy-start | bytes 100
Sparse Core Ops, SparseCore 0:
  9.5 32.9 all-gather.1
  68.2 20.3 all-reduce.4
where the time goes:
time: 168 us
  blocking collectives  78.2 us (47%)
  waiting for transfers between devices  26.1 us (16%)
  other arithmetic  25.9 us (15%)
  matrix products  19.2 us (11%)
  between operations  17.2 us (10%)
    psum x1, blocking collectives, on_device(): lax.psum((jnp.sum(jnp.exp(capped), axis=1), jnp.sum(jnp.where(hits, cappe...  32.7 us
    mul x1, other arithmetic, dequant_down(): grouped = codes.reshape(scales.shape[0], -1, cols) * scales[:, None, :]  17.8 us
    all_gather x1, waiting for transfers between devices, on_device(): lax.all_gather(hidden, 'fsdp', axis=0, tiled=True)  16.6 us
    dot_general x1, matrix products, on_device(): jnp.dot(lax.all_gather(hidden, 'fsdp', axis=0, tiled=True), local_weight,...  15.8 us
    all_gather x1, blocking collectives, on_device(): lax.all_gather(states, ('fsdp', 'sub'), axis=0, tiled=True)  15.1 us
    psum x1, blocking collectives, on_device(): lax.psum((jnp.sum(token_loss), jnp.sum(weights)), ('fsdp', 'sub'))  14.2 us
    all_to_all x1, blocking collectives, on_device(): lax.all_to_all(partial_cols, 'fsdp', split_axis=0, concat_axis=1, tiled=T...  9.71 us
    psum x1, waiting for transfers between devices, normalize_rows(): ffn = lax.psum(ffn, 'mp')  8.84 us
  transfers between devices with their start and end apart: 2, of which 2 were waited for; matrix products, arithmetic and copies ran while one was open for 13% of the time, Pallas kernels for 0%

commit v1 on v0

--- a/solution.py
+++ b/solution.py
@@ -28,7 +28,8 @@
 
 
 def normalize_rows(ffn, residual, post_gain, final_gain):
-    ffn = lax.psum(ffn, "mp")
+    terms = lax.all_gather(ffn, "mp", axis=0, tiled=False)
+    ffn = terms.sum(axis=0)
     normed = ffn * lax.rsqrt(jnp.mean(ffn * ffn, axis=-1, keepdims=True) + EPS) * post_gain
     stream = residual.astype(jnp.float32) + normed
     return (

time: 168 us -> 159 us (0.946)
  waiting for transfers between devices: 26.1 us -> 17.3 us
  starting transfers between devices: 0.08 us -> 3.5 us
  other arithmetic: 25.9 us -> 23.2 us
  blocking collectives: 78.2 us -> 75.6 us
  matrix products: 19.2 us -> 21.1 us
    all_to_all x1 -> x0, blocking collectives: 9.71 us -> none  [on_device(): lax.all_to_all(partial_cols, 'fsdp', split_axis=0, concat_axis=1, tiled=T...]
    psum x1 -> x0, waiting for transfers between devices: 8.84 us -> none  [normalize_rows(): ffn = lax.psum(ffn, 'mp')]
    all_gather x0 -> x1, blocking collectives: none -> 5.81 us  [normalize_rows(): terms = lax.all_gather(ffn, 'mp', axis=0, tiled=False)]
    all_to_all x0 -> x1, starting transfers between devices: none -> 3.47 us  [on_device(): lax.all_to_all(partial_cols, 'fsdp', split_axis=0, concat_axis=1, tiled=T...]
    unnamed x1, blocking collectives: 6.46 us -> 9.34 us
    dot_general x1, matrix products: 15.8 us -> 17.7 us  [on_device(): jnp.dot(lax.all_gather(hidden, 'fsdp', axis=0, tiled=True), local_weight,...]
  transfers between devices with their start and end apart: 2 -> 2, of which waited for: 2 -> 1; matrix products, arithmetic and copies ran while one was open for 13% -> 14% of each run, Pallas kernels for 0% -> 0%
where the time goes in v1:
time: 159 us
  blocking collectives  75.6 us (48%)
  other arithmetic  23.2 us (15%)
  matrix products  21.1 us (13%)
  waiting for transfers between devices  17.3 us (11%)
  between operations  17.2 us (11%)
  starting transfers between devices  3.5 us (2%)
    psum x1, blocking collectives, on_device(): lax.psum((jnp.sum(jnp.exp(capped), axis=1), jnp.sum(jnp.where(hits, cappe...  31.2 us
    mul x1, other arithmetic, dequant_down(): grouped = codes.reshape(scales.shape[0], -1, cols) * scales[:, None, :]  17.8 us
    dot_general x1, matrix products, on_device(): jnp.dot(lax.all_gather(hidden, 'fsdp', axis=0, tiled=True), local_weight,...  17.7 us
    all_gather x1, waiting for transfers between devices, on_device(): lax.all_gather(hidden, 'fsdp', axis=0, tiled=True)  16.6 us
    all_gather x1, blocking collectives, on_device(): lax.all_gather(states, ('fsdp', 'sub'), axis=0, tiled=True)  15 us
    psum x1, blocking collectives, on_device(): lax.psum((jnp.sum(token_loss), jnp.sum(weights)), ('fsdp', 'sub'))  14.2 us
    unnamed x1, blocking collectives  9.34 us
    all_gather x1, blocking collectives, normalize_rows(): terms = lax.all_gather(ffn, 'mp', axis=0, tiled=False)  5.81 us
  transfers between devices with their start and end apart: 2, of which 1 were waited for; matrix products, arithmetic and copies ran while one was open for 14% of the time, Pallas kernels for 0%

profile of v1, /device:TPU:0, one launch (start us, length us, event | category | flops | bytes accessed | tf_op | source)
XLA Modules:
  0.0 159.0 jit_solution(1018941785445668045)
XLA Ops:
  7.2 0.0 all-gather.2.cloned.1.call-start
  7.2 0.7 all-gather.2.cloned.1.call-update
  7.9 0.1 shift_left.49
  8.0 17.8 %fusion.2 = bf16[18432,1152]{1,0:T(8,128)(2,1)} fusion(s32[18432]{0:T(1024)S(1)} %broadcast_bitcast_fusion, s32[2304,1152]{1,0:T(8,128)} %param.12, bf16[144,1152]{1,0:T(8,128)(2,1)} %param.13), kind=kLoop, calls=%fused_computation.3 | loop fusion | flops 148635648 | bytes 53489664 | tf_op jit(solution)/shard_map/mul | solution.py:19
  25.9 0.0 copy-start.7
  25.9 0.0 copy-start.6
  25.9 0.0 copy-start
  25.9 0.0 copy-start.3
  25.9 0.0 copy-start.1
  25.9 0.0 copy-start.2
  25.9 0.0 copy-start.4
  25.9 16.6 %all-gather.2.cloned.1.call-done = bf16[32,18432]{1,0:T(8,128)(2,1)} async-done(((bf16[8,18432]{1,0:T(8,128)(2,1)}), bf16[32,18432]{1,0:T(8,128)(2,1)}) %all-gather.2.cloned.1.call-update) | async-done | bytes 1179664 | tf_op jit(solution)/shard_map/all_gather | solution.py:55
  42.6 17.7 %convolution_bitcast_fusion = f32[4,8,1152]{2,1,0:T(8,128)} fusion(bf16[32,18432]{1,0:T(8,128)(2,1)} %all-gather.2.cloned.1.call-done, bf16[18432,1152]{1,0:T(8,128)(2,1)} %fusion.2), kind=kOutput, calls=%fused_computation.8 | convolution fusion | flops 1358954496 | bytes 43794432 | tf_op jit(solution)/shard_map/dot_general | solution.py:54
  60.3 0.0 copy-start.5
  60.3 3.5 %all-to-all-start = ((f32[4,8,1152]{2,1,0:T(8,128)}), f32[4,8,1152]{2,1,0:T(8,128)S(1)}, u32[]{:S(2)}, u32[]{:S(2)}) async-start(f32[4,8,1152]{2,1,0:T(8,128)} %convolution_bitcast_fusion), calls=%async_computation | async-start | bytes 294912 | tf_op jit(solution)/shard_map/all_to_all | solution.py:59
  63.8 0.1 shift_left.56
  63.8 0.1 shift_left.57
  63.9 0.0 copy-done.7
  63.9 0.6 dynamic-slice
  65.2 0.0 copy-done.6
  65.2 0.2 dynamic-update-slice
  65.4 0.0 copy-done
  65.4 0.0 copy-done.3
  65.4 3.6 %fusion.5 = bf16[512,4608]{0,1:T(8,128)(2,1)} fusion(s32[4608]{0:T(1024)S(1)} %shift_left.57, s32[512,576]{0,1:T(8,128)S(1)} %copy-done, bf16[512,36]{0,1:T(8,128)(2,1)S(1)} %copy-done.3), kind=kLoop, calls=%fused_computation.7 | loop fusion | flops 16515072 | bytes 5953536 | tf_op jit(solution)/shard_map/mul | solution.py:26
  69.0 9.3 %all-reduce = s32[64]{0:T(128)S(1)} all-reduce(s32[64]{0:T(128)S(1)} %dynamic-update-slice), channel_id=1, replica_groups=mesh['groups'=2,'fsdp'=4,'mp'=2,'sub'=2] {'fsdp','sub'}, use_global_device_ids=true, to_apply=%add | all-reduce | flops 64 | bytes 512
  78.3 0.0 all-to-all-done
  78.3 5.8 %all_gather.17 = f32[2,8,4608]{2,1,0:T(8,128)S(1)} all-gather(f32[1,8,4608]{2,1,0:T(8,128)S(1)} %bitcast.35), channel_id=1, replica_groups=mesh['groups'=2,'fsdp'=4,'mp'=2,'sub'=2] {'mp'}, dimensions={0}, use_global_device_ids=true | all-gather | bytes 442368 | tf_op jit(solution)/shard_map/all_gather | solution.py:31
  84.2 0.2 multiply_reduce_fusion.1
  84.3 0.0 copy-done.1
  84.3 0.0 copy-done.2
  84.3 0.2 multiply_reduce_fusion
  84.6 0.0 copy-done.4
  84.6 0.1 multiply_convert_fusion
  84.7 15.0 %all_gather.18 = bf16[64,4608]{1,0:T(8,128)(2,1)S(1)} all-gather(bf16[8,4608]{1,0:T(8,128)(2,1)S(1)} %multiply_convert_fusion), channel_id=1, replica_groups=mesh['groups'=2,'fsdp'=4,'mp'=2,'sub'=2] {'fsdp','sub'}, dimensions={0}, use_global_device_ids=true | all-gather | bytes 663552 | tf_op jit(solution)/shard_map/all_gather | solution.py:62
  99.7 3.4 %exponential_reduce_fusion = (f32[64]{0:T(128)S(1)}, f32[64]{0:T(128)S(1)}) fusion(s32[512]{0:T(512)S(1)} %iota_add_fusion, s32[64]{0:T(128)S(1)} %all-reduce, bf16[64,4608]{1,0:T(8,128)(2,1)S(1)} %all_gather.18, bf16[512,4608]{0,1:T(8,128)(2,1)} %fusion.5), kind=kOutput, calls=%fused_computation.17 | convolution fusion | flops 302186368 | bytes 5311232 | tf_op jit(solution)/shard_map/dot_general | solution.py:66
  103.1 31.2 %all-reduce.1 = (f32[64]{0:T(128)S(1)}, f32[64]{0:T(128)S(1)}) all-reduce(f32[64]{0:T(128)S(1)} %get-tuple-element.3, f32[64]{0:T(128)S(1)} %get-tuple-element.2), channel_id=1, replica_groups=mesh['groups'=2,'fsdp'=4,'mp'=2,'sub'=2] {'fsdp','mp','sub'}, use_global_device_ids=true, to_apply=%region_6.7 | all-reduce | flops 128 | bytes 1024 | tf_op jit(solution)/shard_map/psum | solution.py:74
  134.3 0.0 copy-done.5
  134.3 1.3 fusion.8
  135.6 14.2 %all-reduce.2 = (f32[]{:T(128)}, f32[]{:T(128)}) all-reduce(f32[]{:T(128)} %get-tuple-element.8, f32[]{:T(128)} %get-tuple-element.10), channel_id=1, replica_groups=mesh['groups'=2,'fsdp'=4,'mp'=2,'sub'=2] {'fsdp','sub'}, use_global_device_ids=true, to_apply=%region_8.9 | all-reduce | flops 2 | bytes 16 | tf_op jit(solution)/shard_map/psum | solution.py:83
  (8 shorter events, 0.1 us)
Async XLA Ops:
  7.2 35.4 %all-gather.2.cloned.1.call-start = ((), (), s32[]{:S(2)}) async-start(), calls=%async_computation.1 | async-start | bytes 1474560 | tf_op jit(solution)/shard_map/all_gather | solution.py:55
  25.9 38.0 %copy-start.7 = (u32[32]{0:T(128)S(1)}, u32[32]{0:T(128)}, u32[]{:S(2)}) copy-start(u32[32]{0:T(128)} %constant.48) | copy-start | bytes 388
  25.9 39.3 %copy-start.6 = (s32[8]{0:T(128)S(1)}, s32[8]{0:T(128)}, u32[]{:S(2)}) copy-start(s32[8]{0:T(128)} %param.18) | copy-start | bytes 100
  25.9 39.5 %copy-start = (s32[512,576]{0,1:T(8,128)S(1)}, s32[512,576]{0,1:T(8,128)}, u32[]{:S(2)}) copy-start(s32[512,576]{0,1:T(8,128)} %param.16) | copy-start | bytes 3538948
  25.9 39.5 %copy-start.3 = (bf16[512,36]{0,1:T(8,128)(2,1)S(1)}, bf16[512,36]{0,1:T(8,128)(2,1)}, u32[]{:S(2)}) copy-start(bf16[512,36]{0,1:T(8,128)(2,1)} %param.17) | copy-start | bytes 110596
  25.9 58.4 %copy-start.1 = (bf16[8,4608]{1,0:T(8,128)(2,1)S(1)}, bf16[8,4608]{1,0:T(8,128)(2,1)}, u32[]{:S(2)}) copy-start(bf16[8,4608]{1,0:T(8,128)(2,1)} %param.11) | copy-start | bytes 221188
  25.9 58.4 %copy-start.2 = (f32[4608]{0:T(1024)S(1)}, f32[4608]{0:T(1024)}, u32[]{:S(2)}) copy-start(f32[4608]{0:T(1024)} %param.14) | copy-start | bytes 55300
  25.9 58.6 %copy-start.4 = (f32[4608]{0:T(1024)S(1)}, f32[4608]{0:T(1024)}, u32[]{:S(2)}) copy-start(f32[4608]{0:T(1024)} %param.15) | copy-start | bytes 55300
  60.3 74.1 %copy-start.5 = (s32[8]{0:T(128)S(1)}, s32[8]{0:T(128)}, u32[]{:S(2)}) copy-start(s32[8]{0:T(128)} %param.19) | copy-start | bytes 100
  60.3 18.1 %all-to-all-start = ((f32[4,8,1152]{2,1,0:T(8,128)}), f32[4,8,1152]{2,1,0:T(8,128)S(1)}, u32[]{:S(2)}, u32[]{:S(2)}) async-start(f32[4,8,1152]{2,1,0:T(8,128)} %convolution_bitcast_fusion), calls=%async_computation | async-start | bytes 294912 | tf_op jit(solution)/shard_map/all_to_all | solution.py:59
Sparse Core Ops, SparseCore 0:
  9.5 32.9 all-gather.1
